TPU v7x, 32 devices: a whole 2x2x4 slice. The times are simulated.
32 devices in a mesh: dp: 4 (over y, core), wide: 8 (over z, x).
Axes of the slice: x: 2, y: 2, z: 4, core: 2. Of those that a mesh axis runs over, the one named last changes fastest.
Arguments:
- fields: bfloat16 [16, 64, 128, 1280], P('dp', 'wide'), may hold values from -6 to 6
- targets: bfloat16 [16, 64, 128, 1280], P('dp', 'wide'), may hold values from -6 to 6
- patch_mask: int32 [16, 64, 128], P('dp', 'wide'), may hold values from 0 to 1, as said below
- channel_mask: int32 [16, 20], P('dp'), may hold values from 0 to 1, as said below
- embed_weight: float32 [1280, 768], P(('dp', 'wide')), may hold values from -0.15625 to 0.15625
- head_weight: float32 [768, 1280], P(('dp', 'wide')), may hold values from -0.21875 to 0.21875
- expand_weight: float32 [768, 3072], P(('dp', 'wide')), may hold values from -0.21875 to 0.21875
- project_weight: float32 [3072, 768], P(('dp', 'wide')), may hold values from -0.109375 to 0.109375
- spectral_weight: float32 [2, 2, 768, 96], P(None, None, ('dp', 'wide')), may hold values from -0.4375 to 0.4375
- small_params: float32 [14, 768], P(None, ('dp', 'wide')), may hold values from -1.2 to 1.3
- embed_moment: float32 [1280, 768], P(('dp', 'wide'))
- head_moment: float32 [768, 1280], P(('dp', 'wide'))
- expand_moment: float32 [768, 3072], P(('dp', 'wide'))
- project_moment: float32 [3072, 768], P(('dp', 'wide'))
- spectral_moment: float32 [2, 2, 768, 96], P(None, None, ('dp', 'wide'))
- small_moment: float32 [14, 768], P(None, ('dp', 'wide'))
- embed_square: float32 [1280, 768], P(('dp', 'wide'))
- head_square: float32 [768, 1280], P(('dp', 'wide'))
- expand_square: float32 [768, 3072], P(('dp', 'wide'))
- project_square: float32 [3072, 768], P(('dp', 'wide'))
- spectral_square: float32 [2, 2, 768, 96], P(None, None, ('dp', 'wide'))
- small_square: float32 [14, 768], P(None, ('dp', 'wide'))
Outputs:
- loss: float32 [], replicated
- grad_norm: float32 [], replicated
- embed_next: float32 [1280, 768], P(('dp', 'wide'))
- embed_moment_next: float32 [1280, 768], P(('dp', 'wide'))
- embed_square_next: float32 [1280, 768], P(('dp', 'wide'))
- head_next: float32 [768, 1280], P(('dp', 'wide'))
- head_moment_next: float32 [768, 1280], P(('dp', 'wide'))
- head_square_next: float32 [768, 1280], P(('dp', 'wide'))
- expand_next: float32 [768, 3072], P(('dp', 'wide'))
- expand_moment_next: float32 [768, 3072], P(('dp', 'wide'))
- expand_square_next: float32 [768, 3072], P(('dp', 'wide'))
- project_next: float32 [3072, 768], P(('dp', 'wide'))
- project_moment_next: float32 [3072, 768], P(('dp', 'wide'))
- project_square_next: float32 [3072, 768], P(('dp', 'wide'))
- spectral_next: float32 [2, 2, 768, 96], P(None, None, ('dp', 'wide'))
- spectral_moment_next: float32 [2, 2, 768, 96], P(None, None, ('dp', 'wide'))
- spectral_square_next: float32 [2, 2, 768, 96], P(None, None, ('dp', 'wide'))
- small_next: float32 [14, 768], P(None, ('dp', 'wide'))
- small_moment_next: float32 [14, 768], P(None, ('dp', 'wide'))
- small_square_next: float32 [14, 768], P(None, ('dp', 'wide'))
Inputs may be any that keep to these rules, and one draw needn't show every extreme that they name: `patch_mask`: A sample of the coarse group other than the first has valid patches only in its first 32 rows and 64 columns; the first grid row of the first sample is all valid. `channel_mask`: the first sample observes every channel.
All inputs are finite; a program needn't handle non-finite values.
Results may differ from a plain program's by a relative error of at most 0.0055.
The roundings to bfloat16 on the way count: a program that leaves them out, or rounds other values in their place, can miss the bound.
Values may be sent and summed in bfloat16 or wider, within the bound.
A program may use at most 512 MiB of HBM per device.

v0:
```python
import jax
import jax.numpy as jnp
from jax import lax
from jax.sharding import PartitionSpec as P

EPSILON = 1e-06
SHRINK = 0.01
BETA_ONE = 0.9
BETA_TWO = 0.95
RATES = (0.08, 0.1, 0.1, 0.05, 0.3, 0.5)
DECAYS = (0.1, 0.1, 0.1, 0.1, 0.1, 0.0)


def layer_norm(values, gain, shift):
    centred = values - jnp.mean(values, axis=-1, keepdims=True)
    spread = jnp.mean(centred * centred, axis=-1, keepdims=True)
    return centred * lax.rsqrt(spread + EPSILON) * gain + shift


def make_tables(grid_height, grid_width):
    across = jnp.arange(grid_width, dtype=jnp.int32)
    freqs = jnp.arange(grid_width // 2, dtype=jnp.int32)
    angles = (
        2.0
        * jnp.pi
        / grid_width
        * (across[:, None] * freqs[None, :] % grid_width).astype(jnp.float32)
    )
    row_table = (
        jnp.stack([jnp.cos(angles), -jnp.sin(angles)], axis=1) / jnp.sqrt(jnp.float32(grid_width))
    ).astype(jnp.bfloat16)
    doubling = jnp.where(freqs == 0, 1.0, 2.0).astype(jnp.float32)
    inv_table = (row_table.astype(jnp.float32) * doubling).astype(jnp.bfloat16)
    down = jnp.arange(grid_height, dtype=jnp.int32)
    col_angles = (
        2.0
        * jnp.pi
        / grid_height
        * (down[:, None] * down[None, :] % grid_height).astype(jnp.float32)
    )
    cosine = jnp.cos(col_angles) / jnp.sqrt(jnp.float32(grid_height))
    sine = jnp.sin(col_angles) / jnp.sqrt(jnp.float32(grid_height))
    col_table = jnp.stack([jnp.stack([cosine, sine]), jnp.stack([-sine, cosine])]).astype(
        jnp.bfloat16
    )
    return (row_table, inv_table, col_table)


def complex_mix(spec, weight, bias):
    shape = spec.shape
    block_size = weight.shape[2]
    nblocks = weight.shape[1] // block_size
    blocks = spec.reshape(-1, 2, shape[-2], nblocks, block_size)
    kernel = weight.reshape(2, nblocks, block_size, block_size)
    prods = jnp.einsum("xakbi,cbij->xackbj", blocks, kernel, preferred_element_type=jnp.float32)
    real_part = prods[:, 0, 0] - prods[:, 1, 1]
    imag_part = prods[:, 0, 1] + prods[:, 1, 0]
    return jnp.stack([real_part, imag_part], axis=1).reshape(shape) + bias[:, None, :]


def complex_back(grad_out, spec, weight):
    shape = spec.shape
    block_size = weight.shape[2]
    nblocks = weight.shape[1] // block_size
    blocks = spec.reshape(-1, 2, shape[-2], nblocks, block_size)
    grads_blocks = grad_out.reshape(-1, 2, shape[-2], nblocks, block_size)
    kernel = weight.reshape(2, nblocks, block_size, block_size)
    prods = jnp.einsum(
        "xokbj,cbij->xockbi", grads_blocks, kernel, preferred_element_type=jnp.float32
    )
    real_part = prods[:, 0, 0] + prods[:, 1, 1]
    imag_part = prods[:, 1, 0] - prods[:, 0, 1]
    grad_spec = jnp.stack([real_part, imag_part], axis=1).reshape(shape)
    cross = jnp.einsum(
        "xakbi,xokbj->aobij", blocks, grads_blocks, preferred_element_type=jnp.float32
    )
    grad_weight = jnp.stack([cross[0, 0] + cross[1, 1], cross[0, 1] - cross[1, 0]]).reshape(
        weight.shape
    )
    grad_bias = jnp.sum(
        grad_out.reshape(-1, 2, shape[-2], shape[-1]), axis=(0, 2), dtype=jnp.float32
    )
    return (grad_spec, grad_weight, grad_bias)


def forward_layer(inputs, used, tables, layout):
    embed_used, head_used, expand_used, project_used, spectral_used, small_used = used
    row_table, inv_table, col_table = tables
    samples, rows_dev, grid_width = layout
    tokens = inputs.shape[0]
    width_model = embed_used.shape[1]
    hidden_zero = jnp.dot(inputs, embed_used, preferred_element_type=jnp.float32) + small_used[4]
    normed_one = layer_norm(hidden_zero, small_used[0], small_used[1])
    normed_low = normed_one.astype(jnp.bfloat16).reshape(samples, rows_dev, grid_width, width_model)
    rows_freq = jnp.einsum(
        "srwd,wak->srakd", normed_low, row_table, preferred_element_type=jnp.float32
    ).astype(jnp.bfloat16)
    rows_moved = lax.all_to_all(rows_freq, "wide", split_axis=3, concat_axis=1, tiled=True)
    spectrum = jnp.einsum(
        "oaxi,siakd->sxokd", col_table, rows_moved, preferred_element_type=jnp.float32
    ).astype(jnp.bfloat16)
    first_pre = complex_mix(spectrum, spectral_used[0], small_used[10:12])
    first_act = jax.nn.relu(first_pre).astype(jnp.bfloat16)
    second_pre = complex_mix(first_act, spectral_used[1], small_used[12:14])
    shrunk = (second_pre - jnp.clip(second_pre, -SHRINK, SHRINK)).astype(jnp.bfloat16)
    back_cols = jnp.einsum(
        "aoxi,sxakd->siokd", col_table, shrunk, preferred_element_type=jnp.float32
    ).astype(jnp.bfloat16)
    cols_moved = lax.all_to_all(back_cols, "wide", split_axis=1, concat_axis=3, tiled=True)
    filtered = jnp.einsum(
        "wak,srakd->srwd", inv_table, cols_moved, preferred_element_type=jnp.float32
    ).reshape(tokens, width_model)
    hidden_one = hidden_zero + filtered + normed_one
    normed_two = layer_norm(hidden_one, small_used[2], small_used[3]).astype(jnp.bfloat16)
    expand_pre = jnp.dot(normed_two, expand_used, preferred_element_type=jnp.float32) + small_used[
        6:10
    ].reshape(-1)
    expand_act = jax.nn.gelu(expand_pre, approximate=False).astype(jnp.bfloat16)
    hidden_two = (
        hidden_one
        + jnp.dot(expand_act, project_used, preferred_element_type=jnp.float32)
        + small_used[5]
    )
    hidden_low = hidden_two.astype(jnp.bfloat16)
    predict = jnp.dot(hidden_low, head_used, preferred_element_type=jnp.float32)
    kept = (
        hidden_zero,
        spectrum,
        first_pre,
        first_act,
        second_pre,
        hidden_one,
        normed_two,
        expand_pre,
        expand_act,
        hidden_low,
    )
    return (predict, kept)


def backward_layer(grad_predict, inputs, used, tables, layout, kept):
    embed_used, head_used, expand_used, project_used, spectral_used, small_used = used
    row_table, inv_table, col_table = tables
    samples, rows_dev, grid_width = layout
    (
        hidden_zero,
        spectrum,
        first_pre,
        first_act,
        second_pre,
        hidden_one,
        normed_two,
        expand_pre,
        expand_act,
        hidden_low,
    ) = kept
    tokens = inputs.shape[0]
    width_model = embed_used.shape[1]
    grad_low = grad_predict.astype(jnp.bfloat16)
    grad_head = jnp.einsum("td,tp->dp", hidden_low, grad_low, preferred_element_type=jnp.float32)
    grad_two = jnp.einsum("tp,dp->td", grad_low, head_used, preferred_element_type=jnp.float32)
    grad_branch = grad_two.astype(jnp.bfloat16)
    grad_project = jnp.einsum(
        "tf,td->fd", expand_act, grad_branch, preferred_element_type=jnp.float32
    )
    bias_project = jnp.sum(grad_branch, axis=0, dtype=jnp.float32)
    grad_act = jnp.einsum(
        "td,fd->tf", grad_branch, project_used, preferred_element_type=jnp.float32
    )
    gelu_pull = jax.vjp(lambda values: jax.nn.gelu(values, approximate=False), expand_pre)[1]
    grad_pre = gelu_pull(grad_act)[0].astype(jnp.bfloat16)
    grad_expand = jnp.einsum("td,tf->df", normed_two, grad_pre, preferred_element_type=jnp.float32)
    bias_expand = jnp.sum(grad_pre, axis=0, dtype=jnp.float32)
    grad_normed = jnp.einsum("tf,df->td", grad_pre, expand_used, preferred_element_type=jnp.float32)
    second_pull = jax.vjp(layer_norm, hidden_one, small_used[2], small_used[3])[1]
    back_one, gain_two, shift_two = second_pull(grad_normed)
    grad_one = grad_two + back_one
    grad_filter = grad_one.astype(jnp.bfloat16).reshape(samples, rows_dev, grid_width, width_model)
    grad_cols = jnp.einsum(
        "wak,srwd->srakd", inv_table, grad_filter, preferred_element_type=jnp.float32
    ).astype(jnp.bfloat16)
    grad_moved = lax.all_to_all(grad_cols, "wide", split_axis=3, concat_axis=1, tiled=True)
    grad_shrunk = jnp.einsum(
        "aoxi,siokd->sxakd", col_table, grad_moved, preferred_element_type=jnp.float32
    )
    grad_second = jnp.where(jnp.abs(second_pre) > SHRINK, grad_shrunk, 0.0).astype(jnp.bfloat16)
    grad_first_act, weight_two, bias_two = complex_back(grad_second, first_act, spectral_used[1])
    grad_first = jnp.where(first_pre > 0.0, grad_first_act, 0.0).astype(jnp.bfloat16)
    grad_spectrum, weight_one, bias_one = complex_back(grad_first, spectrum, spectral_used[0])
    grad_rows = jnp.einsum(
        "oaxi,sxokd->siakd",
        col_table,
        grad_spectrum.astype(jnp.bfloat16),
        preferred_element_type=jnp.float32,
    ).astype(jnp.bfloat16)
    grad_back = lax.all_to_all(grad_rows, "wide", split_axis=1, concat_axis=3, tiled=True)
    grad_normed_one = (
        jnp.einsum(
            "wak,srakd->srwd", row_table, grad_back, preferred_element_type=jnp.float32
        ).reshape(tokens, width_model)
        + grad_one
    )
    first_pull = jax.vjp(layer_norm, hidden_zero, small_used[0], small_used[1])[1]
    back_zero, gain_one, shift_one = first_pull(grad_normed_one)
    grad_zero = (grad_one + back_zero).astype(jnp.bfloat16)
    grad_embed = jnp.einsum("tp,td->pd", inputs, grad_zero, preferred_element_type=jnp.float32)
    bias_embed = jnp.sum(grad_zero, axis=0, dtype=jnp.float32)
    grad_spectral = jnp.stack([weight_one, weight_two])
    grad_small = jnp.concatenate(
        [
            jnp.stack([gain_one, shift_one, gain_two, shift_two, bias_embed, bias_project]),
            bias_expand.reshape(4, width_model),
            bias_one,
            bias_two,
        ],
        axis=0,
    )
    return (
        lax.psum_scatter(grad_embed, ("dp", "wide"), scatter_dimension=0, tiled=True),
        lax.psum_scatter(grad_head, ("dp", "wide"), scatter_dimension=0, tiled=True),
        lax.psum_scatter(grad_expand, ("dp", "wide"), scatter_dimension=0, tiled=True),
        lax.psum_scatter(grad_project, ("dp", "wide"), scatter_dimension=0, tiled=True),
        lax.psum_scatter(grad_spectral, ("dp", "wide"), scatter_dimension=2, tiled=True),
        lax.psum_scatter(grad_small, ("dp", "wide"), scatter_dimension=1, tiled=True),
    )


def adam_update(master, moment, square, grad, factor, rate, decay):
    clipped = grad * factor
    moment_next = BETA_ONE * moment + (1.0 - BETA_ONE) * clipped
    square_next = BETA_TWO * square + (1.0 - BETA_TWO) * clipped * clipped
    ratio = (
        moment_next / (1.0 - BETA_ONE**10) / (jnp.sqrt(square_next / (1.0 - BETA_TWO**10)) + 1e-08)
    )
    return (master - rate * (ratio + decay * master), moment_next, square_next)


def shards(
    fields,
    targets,
    patch_mask,
    channel_mask,
    embed_weight,
    head_weight,
    expand_weight,
    project_weight,
    spectral_weight,
    small_params,
    embed_moment,
    head_moment,
    expand_moment,
    project_moment,
    spectral_moment,
    small_moment,
    embed_square,
    head_square,
    expand_square,
    project_square,
    spectral_square,
    small_square,
):
    masters = (
        embed_weight,
        head_weight,
        expand_weight,
        project_weight,
        spectral_weight,
        small_params,
    )
    moments = (
        embed_moment,
        head_moment,
        expand_moment,
        project_moment,
        spectral_moment,
        small_moment,
    )
    squares = (
        embed_square,
        head_square,
        expand_square,
        project_square,
        spectral_square,
        small_square,
    )
    gathered = (
        lax.all_gather(embed_weight.astype(jnp.bfloat16), ("dp", "wide"), axis=0, tiled=True),
        lax.all_gather(head_weight.astype(jnp.bfloat16), ("dp", "wide"), axis=0, tiled=True),
        lax.all_gather(expand_weight.astype(jnp.bfloat16), ("dp", "wide"), axis=0, tiled=True),
        lax.all_gather(project_weight.astype(jnp.bfloat16), ("dp", "wide"), axis=0, tiled=True),
        lax.all_gather(spectral_weight.astype(jnp.bfloat16), ("dp", "wide"), axis=2, tiled=True),
        lax.all_gather(small_params.astype(jnp.bfloat16), ("dp", "wide"), axis=1, tiled=True),
    )
    used = tuple(gathered[:5]) + (gathered[5].astype(jnp.float32),)
    samples, rows_dev, grid_width, patch_dim = fields.shape
    grid_height = rows_dev * lax.axis_size("wide")
    tables = make_tables(grid_height, grid_width)
    layout = (samples, rows_dev, grid_width)
    channels = channel_mask.shape[1]
    pixels = patch_dim // channels
    tokens = samples * rows_dev * grid_width
    valid_patch = patch_mask.astype(jnp.float32)
    channel_on = channel_mask.astype(jnp.float32)
    local_counts = jnp.sum(channel_on * jnp.sum(valid_patch, axis=(1, 2))[:, None], axis=0) * pixels
    counts = lax.psum(local_counts, ("dp", "wide"))
    scale_cols = jnp.repeat(1.0 / (channels * counts), pixels)
    inputs = (fields * patch_mask[..., None].astype(jnp.bfloat16)).reshape(tokens, patch_dim)
    predict, kept = forward_layer(inputs, used, tables, layout)
    weighted = (
        valid_patch[..., None] * jnp.repeat(channel_on, pixels, axis=1)[:, None, None, :]
    ).reshape(tokens, patch_dim)
    errors = predict - targets.reshape(tokens, patch_dim).astype(jnp.float32)
    grad_predict = 2.0 * errors * weighted * scale_cols
    reduced = backward_layer(grad_predict, inputs, used, tables, layout, kept)
    local_square = sum((jnp.sum(grad * grad) for grad in reduced))
    local_error = jnp.sum(
        (errors * errors * weighted).reshape(tokens, channels, pixels), axis=(0, 2)
    )
    total_square, error_sums = lax.psum((local_square, local_error), ("dp", "wide"))
    grad_norm = jnp.sqrt(total_square)
    loss = jnp.sum(error_sums / counts) / channels
    batch = samples * lax.axis_size("dp")
    clip_level = 0.25 / jnp.sqrt(jnp.float32(batch * grid_height * grid_width))
    factor = jnp.minimum(1.0, clip_level / grad_norm)
    results = [loss, grad_norm]
    for index in range(6):
        results.extend(
            adam_update(
                masters[index],
                moments[index],
                squares[index],
                reduced[index],
                factor,
                RATES[index],
                DECAYS[index],
            )
        )
    return tuple(results)


def solution(mesh):
    placed = (
        P("dp", "wide", None, None),
        P("dp", "wide", None, None),
        P("dp", "wide", None),
        P("dp", None),
        P(("dp", "wide"), None),
        P(("dp", "wide"), None),
        P(("dp", "wide"), None),
        P(("dp", "wide"), None),
        P(None, None, ("dp", "wide"), None),
        P(None, ("dp", "wide")),
        P(("dp", "wide"), None),
        P(("dp", "wide"), None),
        P(("dp", "wide"), None),
        P(("dp", "wide"), None),
        P(None, None, ("dp", "wide"), None),
        P(None, ("dp", "wide")),
        P(("dp", "wide"), None),
        P(("dp", "wide"), None),
        P(("dp", "wide"), None),
        P(("dp", "wide"), None),
        P(None, None, ("dp", "wide"), None),
        P(None, ("dp", "wide")),
    )
    return jax.shard_map(
        shards,
        mesh=mesh,
        in_specs=placed,
        out_specs=(
            P(),
            P(),
            P(("dp", "wide"), None),
            P(("dp", "wide"), None),
            P(("dp", "wide"), None),
            P(("dp", "wide"), None),
            P(("dp", "wide"), None),
            P(("dp", "wide"), None),
            P(("dp", "wide"), None),
            P(("dp", "wide"), None),
            P(("dp", "wide"), None),
            P(("dp", "wide"), None),
            P(("dp", "wide"), None),
            P(("dp", "wide"), None),
            P(None, None, ("dp", "wide"), None),
            P(None, None, ("dp", "wide"), None),
            P(None, None, ("dp", "wide"), None),
            P(None, ("dp", "wide")),
            P(None, ("dp", "wide")),
            P(None, ("dp", "wide")),
        ),
        check_vma=False,
    )
```

profile of v0, /device:TPU:0, one launch (start us, length us, event | category | flops | bytes accessed | tf_op | source)
XLA Modules:
  0.0 1966.7 jit_solution(1096114445009783065)
XLA Ops:
  9.5 70.5 %all-gather = bf16[32,24,14]{1,2,0:T(8,128)(2,1)S(1)} all-gather(bf16[1,24,14]{1,2,0:T(8,128)(2,1)S(1)} %convert_bitcast_fusion.3), channel_id=1, replica_groups=mesh['dp'=4,'wide'=8] {'dp','wide'}, dimensions={0}, use_global_device_ids=true | all-gather | bytes 22176 | tf_op jit(solution)/shard_map/all_gather | solution.py:292
  124.3 215.2 %all_gather.20 = bf16[2,2,768,96]{3,2,1,0:T(8,128)(2,1)S(1)} all-gather(bf16[2,2,24,96]{3,2,1,0:T(8,128)(2,1)S(1)} %convert_element_type.190), channel_id=1, replica_groups=mesh['dp'=4,'wide'=8] {'dp','wide'}, dimensions={2}, use_global_device_ids=true | all-gather | bytes 608256 | tf_op jit(solution)/shard_map/all_gather | solution.py:291
  353.2 15.2 reshape.647
  368.5 22.8 %convolution_bitcast_fusion.3 = f32[256,2,2,8,8,96]{0,5,2,3,1,4:T(8,128)} fusion(bf16[256,2,8,8,96,1]{4,3,2,1,0,5:T(8,128)(2,1)} %bitcast.304, bf16[2,8,96,96,1,1]{3,2,1,0,5,4:T(8,128)(2,1)S(1)} %bitcast.320), kind=kOutput, calls=%fused_computation.68 | convolution fusion | flops 1207959552 | bytes 31752192 | tf_op jit(solution)/shard_map/xakbi,cbij->xackbj/dot_general | solution.py:55
  420.4 14.8 slice_subtract_fusion.2
  486.0 15.7 copy.232
  508.3 174.4 %psum.22 = f32[20]{0:T(128)S(1)} all-reduce(f32[20]{0:T(128)S(1)} %broadcast_multiply_fusion.3), channel_id=1, replica_groups=mesh['dp'=4,'wide'=8] {'dp','wide'}, use_global_device_ids=true, to_apply=%region_9.10 | all-reduce | flops 20 | bytes 160 | tf_op jit(solution)/shard_map/psum | solution.py:305
  704.3 135.3 %multiply_convert_fusion = (bf16[4096,3072]{1,0:T(8,128)(2,1)}, f32[4096,3072]{1,0:T(8,128)}, f32[4096,3072]{1,0:T(8,128)}) fusion(f32[3072]{0:T(1024)S(1)} %add.410, bf16[768,3072]{1,0:T(8,128)(2,1)} %all-gather.8.cloned.1.call-done, f32[4096,768]{1,0:T(8,128)} %copy-done.1, f32[768]{0:T(1024)S(1)} %copy-done.81, f32[768]{0:T(1024)S(1)} %copy-done.63, ...), kind=kOutput, calls=%fused_computation.4 | convolution fusion | flops 20173553664 | bytes 143181824 | tf_op jit(solution)/shard_map/dot_general | solution.py:115
  839.7 27.6 %add_convert_fusion.2 = bf16[4096,768]{1,0:T(8,128)(2,1)} fusion(f32[4096,768]{1,0:T(8,128)} %copy-done.1, bf16[4096,3072]{1,0:T(8,128)(2,1)} %get-tuple-element.123, bf16[3072,768]{1,0:T(8,128)(2,1)} %all-gather.10.cloned.1.call-done, f32[768]{0:T(1024)S(1)} %copy-done.83), kind=kOutput, calls=%fused_computation.56 | convolution fusion | flops 19336790016 | bytes 48761856 | tf_op jit(solution)/shard_map/dot_general | solution.py:121
  867.4 16.8 fusion.10
  895.3 54.2 %convert_reduce_fusion = (f32[3072]{0:T(1024)}, bf16[4096,3072]{1,0:T(8,128)(2,1)}) fusion(f32[4096,3072]{1,0:T(8,128)} %get-tuple-element.124, bf16[3072,768]{1,0:T(8,128)(2,1)} %all-gather.10.cloned.1.call-done, f32[4096,768]{1,0:T(8,128)} %fusion.131, f32[4096,3072]{1,0:T(8,128)} %get-tuple-element.150, f32[3072]{0:T(1024)S(1)} %add.410), kind=kOutput, calls=%fused_computation.2 | convolution fusion | flops 19544403968 | bytes 143155200 | tf_op jit(solution)/shard_map/td,fd->tf/dot_general | solution.py:167
  949.5 27.8 %multiply_reduce_fusion = (f32[768]{0:T(1024)}, f32[4096]{0:T(1024)S(1)}, f32[768]{0:T(1024)}, f32[4096,768]{1,0:T(8,128)S(1)}) fusion(f32[4096,768]{1,0:T(8,128)} %copy-done.1, f32[4096]{0:T(1024)S(1)} %fusion.106, f32[4096]{0:T(1024)S(1)} %broadcast_multiply_fusion.1, f32[768]{0:T(1024)S(1)} %copy-done.63, bf16[4096,3072]{1,0:T(8,128)(2,1)} %get-tuple-element.153, ...), kind=kOutput, calls=%fused_computation.49 | convolution fusion | flops 19352514560 | bytes 55108608 | tf_op jit(solution)/shard_map/tf,df->td/dot_general | solution.py:174
  985.0 16.7 fusion.124
  1003.5 15.7 copy.234
  1024.5 13.9 fusion.133
  1038.6 139.2 %all-to-all-done.2 = bf16[4,8,2,64,768]{4,2,1,0,3:T(2,128)(2,1)} async-done(((bf16[4,8,2,64,768]{4,2,1,0,3:T(2,128)(2,1)}), bf16[4,8,2,64,768]{4,2,1,0,3:T(2,128)(2,1)}, u32[]{:S(2)}, u32[]{:S(2)}) %all-to-all-start.2) | async-done | bytes 6291488 | tf_op jit(solution)/shard_map/all_to_all | solution.py:182
  1194.7 15.0 reshape.650
  1209.7 23.2 %fusion.72 = f32[2,2,8,96,96]{3,4,0,1,2:T(8,128)S(1)} fusion(bf16[256,2,8,8,96,1]{4,3,2,1,0,5:T(8,128)(2,1)} %bitcast.302, f32[256,1,8,8,96]{0,4,2,3,1:T(8,128)} %copy-done.2, f32[256,1,8,8,96]{0,4,2,3,1:T(8,128)} %fusion.155, f32[2,8,96]{2,1,0:T(8,128)S(1)} %copy-done.33), kind=kOutput, calls=%fused_computation.122 | convolution fusion | flops 1220542464 | bytes 20060160 | tf_op jit(solution)/shard_map/xakbi,xokbj->aobij/dot_general | solution.py:74
  1233.8 23.0 %convolution_bitcast_fusion.1 = f32[256,2,2,8,8,96]{0,5,3,4,2,1:T(8,128)} fusion(bf16[2,8,96,96,1,1]{3,2,5,1,0,4:T(8,128)(2,1)S(1)} %bitcast.319, bf16[256,2,8,8,96,1]{4,3,2,1,0,5:T(8,128)(2,1)} %bitcast.303), kind=kOutput, calls=%fused_computation.66 | convolution fusion | flops 1207959552 | bytes 31752192 | tf_op jit(solution)/shard_map/xokbj,cbij->xockbi/dot_general | solution.py:68
  1277.2 12.8 fusion.67
  1293.1 29.1 %fusion.110 = f32[3072,768]{1,0:T(8,128)} fusion(bf16[4096,3072]{1,0:T(8,128)(2,1)} %get-tuple-element.123, f32[4096,768]{1,0:T(8,128)} %fusion.131), kind=kOutput, calls=%fused_computation.222 | convolution fusion | flops 19330498560 | bytes 47185920 | tf_op jit(solution)/shard_map/tf,td->fd/dot_general | solution.py:163
  1322.3 13.0 convolution_bitcast_fusion
  1377.7 15.7 copy.247
  1398.2 29.7 %fusion.115 = f32[768,3072]{1,0:T(8,128)} fusion(bf16[4096,3072]{1,0:T(8,128)(2,1)} %get-tuple-element.153, f32[4096,768]{1,0:T(8,128)} %copy-done.1, f32[768]{0:T(1024)S(1)} %copy-done.82, f32[768]{0:T(1024)S(1)} %copy-done.64, f32[4096]{0:T(1024)S(1)} %copy-done.55, f32[4096]{0:T(1024)S(1)} %copy-done.37), kind=kOutput, calls=%fused_computation.227 | convolution fusion | flops 19343081472 | bytes 47224832 | tf_op jit(solution)/shard_map/td,tf->df/dot_general | solution.py:172
  1428.0 114.7 %all-to-all-done.3 = bf16[4,64,2,8,768]{4,2,3,0,1:T(2,128)(2,1)} async-done(((bf16[4,64,2,8,768]{4,2,3,0,1:T(2,128)(2,1)}), bf16[4,64,2,8,768]{4,2,3,0,1:T(2,128)(2,1)}, u32[]{:S(2)}, u32[]{:S(2)}) %all-to-all-start.3) | async-done | bytes 6291488 | tf_op jit(solution)/shard_map/all_to_all | solution.py:196
  1552.7 20.1 %multiply_reduce_fusion.1 = (f32[768]{0:T(1024)S(1)}, f32[4096]{0:T(1024)S(1)}, f32[768]{0:T(1024)S(1)}, f32[4096,768]{1,0:T(8,128)}) fusion(f32[4096,768]{1,0:T(8,128)} %copy-done, f32[4096]{0:T(1024)S(1)} %copy-done.27, f32[4096]{0:T(1024)S(1)} %copy-done.21, f32[768]{0:T(1024)S(1)} %copy-done.43, f32[768]{0:T(1024)S(1)} %copy-done.53, ...), kind=kLoop, calls=%fused_computation.50 | loop fusion | flops 31451648 | bytes 50393088 | tf_op jit(solution)/shard_map/transpose(jvp())/reduce_sum | solution.py:17
  1572.9 12.6 fusion.123
  1637.4 14.8 reduce-scatter.12.cloned.1.call-done
  1653.9 139.4 %reduce-scatter.10.cloned.1.call-done = f32[24,3072]{1,0:T(8,128)} async-done(((f32[768,3072]{1,0:T(8,128)}), f32[24,3072]{1,0:T(8,128)}) %reduce-scatter.10.cloned.1.call-update) | async-done | bytes 294928 | tf_op jit(solution)/shard_map/reduce_scatter | solution.py:221
  1795.2 40.1 %all-reduce.1 = f32[14,768]{1,0:T(8,128)S(1)} all-reduce(f32[14,768]{1,0:T(8,128)S(1)} %concatenate.15), channel_id=7, replica_groups=mesh['dp'=4,'wide'=8] {'dp','wide'}, use_global_device_ids=true, to_apply=%region_34.35.clone | all-reduce | flops 10752 | bytes 86016
  1836.0 66.3 %reduce-scatter.6.cloned.1.call-done = f32[40,768]{1,0:T(8,128)} async-done(((f32[1280,768]{1,0:T(8,128)}), f32[40,768]{1,0:T(8,128)}) %reduce-scatter.6.cloned.1.call-update) | async-done | bytes 122896 | tf_op jit(solution)/shard_map/reduce_scatter | solution.py:219
  1907.7 39.9 %all-reduce.2 = (f32[20]{0:T(128)S(1)}, f32[]{:T(128)}) all-reduce(f32[20]{0:T(128)S(1)} %copy-done.86, f32[]{:T(128)S(6)} %add.436), channel_id=1, replica_groups=mesh['dp'=4,'wide'=8] {'dp','wide'}, use_global_device_ids=true, to_apply=%region_6.7 | all-reduce | flops 21 | bytes 168 | tf_op jit(solution)/shard_map/psum | solution.py:319
  (351 shorter events, 358.2 us)
Async XLA Ops:
  7.2 86.6 %all-gather.6.cloned.1.call-start = ((), (), s32[]{:S(2)}) async-start(), calls=%async_computation.8 | async-start | bytes 2027520 | tf_op jit(solution)/shard_map/all_gather | solution.py:287
  80.6 604.2 %copy-start.17 = (bf16[128,2,64]{0,2,1:T(8,128)(2,1)}, bf16[128,2,64]{0,2,1:T(8,128)(2,1)S(1)}, u32[]{:S(2)}) copy-start(bf16[128,2,64]{0,2,1:T(8,128)(2,1)S(1)} %fusion.84) | copy-start | bytes 98308
  81.2 608.8 %copy-start.42 = (f32[768]{0:T(1024)}, f32[768]{0:T(1024)S(1)}, u32[]{:S(2)}) copy-start(f32[768]{0:T(1024)S(1)} %get-tuple-element.91) | copy-start | bytes 9220
  81.3 608.8 %copy-start.52 = (f32[768]{0:T(1024)}, f32[768]{0:T(1024)S(1)}, u32[]{:S(2)}) copy-start(f32[768]{0:T(1024)S(1)} %get-tuple-element.90) | copy-start | bytes 9220
  105.6 584.5 %copy-start.20 = (f32[4096]{0:T(1024)}, f32[4096]{0:T(1024)S(1)}, u32[]{:S(2)}) copy-start(f32[4096]{0:T(1024)S(1)} %broadcast_multiply_fusion.2) | copy-start | bytes 49156
  107.5 582.6 %copy-start.26 = (f32[4096]{0:T(1024)}, f32[4096]{0:T(1024)S(1)}, u32[]{:S(2)}) copy-start(f32[4096]{0:T(1024)S(1)} %fusion.105) | copy-start | bytes 49156
  118.6 221.3 %all-to-all-start = ((bf16[4,8,2,64,768]{4,1,0,2,3:T(8,128)(2,1)}), bf16[4,8,2,64,768]{4,1,0,2,3:T(8,128)(2,1)}, u32[]{:S(2)}, u32[]{:S(2)}) async-start(bf16[4,8,2,64,768]{4,1,0,2,3:T(8,128)(2,1)} %copy.216), calls=%async_computation | async-start | bytes 12582912 | tf_op jit(solution)/shard_map/all_to_all | solution.py:98
  123.3 580.9 %all-gather.8.cloned.1.call-start = ((), (), s32[]{:S(2)}) async-start(), calls=%async_computation.9 | async-start | bytes 4866048 | tf_op jit(solution)/shard_map/all_gather | solution.py:289
  124.3 359.0 %copy-start.77 = (f32[2,768]{1,0:T(2,128)}, f32[2,768]{1,0:T(2,128)S(1)}, u32[]{:S(2)}) copy-start(f32[2,768]{1,0:T(2,128)S(1)} %get-tuple-element.142) | copy-start | bytes 18436
  501.7 183.1 %all-to-all-start.1 = ((bf16[4,64,2,8,768]{4,2,3,0,1:T(2,128)(2,1)}), bf16[4,64,2,8,768]{4,2,3,0,1:T(2,128)(2,1)}, u32[]{:S(2)}, u32[]{:S(2)}) async-start(bf16[4,64,2,8,768]{4,2,3,0,1:T(2,128)(2,1)} %copy.232), calls=%async_computation.1 | async-start | bytes 12582912 | tf_op jit(solution)/shard_map/all_to_all | solution.py:109
  506.6 333.1 %all-gather.10.cloned.1.call-start = ((), (), s32[]{:S(2)}) async-start(), calls=%async_computation.10 | async-start | bytes 4866048 | tf_op jit(solution)/shard_map/all_gather | solution.py:290
  507.4 360.0 %all-gather.12.cloned.1.call-start = ((), (), s32[]{:S(2)}) async-start(), calls=%async_computation.11 | async-start | bytes 2027520 | tf_op jit(solution)/shard_map/all_gather | solution.py:288
  1019.2 158.6 %all-to-all-start.2 = ((bf16[4,8,2,64,768]{4,2,1,0,3:T(2,128)(2,1)}), bf16[4,8,2,64,768]{4,2,1,0,3:T(2,128)(2,1)}, u32[]{:S(2)}, u32[]{:S(2)}) async-start(bf16[4,8,2,64,768]{4,2,1,0,3:T(2,128)(2,1)} %copy.234), calls=%async_computation.2 | async-start | bytes 12582912 | tf_op jit(solution)/shard_map/all_to_all | solution.py:182
  1024.5 601.3 %reduce-scatter.8.cloned.1.call-start = ((), (), s32[]{:S(2)}) async-start(), calls=%async_computation.13 | async-start | bytes 4055040 | tf_op jit(solution)/shard_map/reduce_scatter | solution.py:220
  1038.5 597.4 %all-reduce.5.cloned.1.call-start = ((), (), s32[]{:S(2)}) async-start(), calls=%async_computation.16 | async-start | bytes 3145728
  1293.1 359.2 %reduce-scatter.12.cloned.1.call-start = ((), (), s32[]{:S(2)}) async-start(), calls=%async_computation.15 | async-start | bytes 9732096 | tf_op jit(solution)/shard_map/reduce_scatter | solution.py:222
  1393.4 149.3 %all-to-all-start.3 = ((bf16[4,64,2,8,768]{4,2,3,0,1:T(2,128)(2,1)}), bf16[4,64,2,8,768]{4,2,3,0,1:T(2,128)(2,1)}, u32[]{:S(2)}, u32[]{:S(2)}) async-start(bf16[4,64,2,8,768]{4,2,3,0,1:T(2,128)(2,1)} %copy.247), calls=%async_computation.3 | async-start | bytes 12582912 | tf_op jit(solution)/shard_map/all_to_all | solution.py:196
  1398.1 395.2 %reduce-scatter.10.cloned.1.call-start = ((), (), s32[]{:S(2)}) async-start(), calls=%async_computation.14 | async-start | bytes 9732096 | tf_op jit(solution)/shard_map/reduce_scatter | solution.py:221
  1428.0 474.3 %reduce-scatter.6.cloned.1.call-start = ((), (), s32[]{:S(2)}) async-start(), calls=%async_computation.12 | async-start | bytes 4055040 | tf_op jit(solution)/shard_map/reduce_scatter | solution.py:219
  1629.9 321.2 %copy-start.23 = (f32[24,1280]{1,0:T(8,128)S(1)}, f32[24,1280]{1,0:T(8,128)}, u32[]{:S(2)}) copy-start(f32[24,1280]{1,0:T(8,128)} %param.27) | copy-start | bytes 368644
  1629.9 321.2 %copy-start.25 = (f32[24,1280]{1,0:T(8,128)S(1)}, f32[24,1280]{1,0:T(8,128)}, u32[]{:S(2)}) copy-start(f32[24,1280]{1,0:T(8,128)} %reduce-scatter.8.cloned.1.call-done) | copy-start | bytes 368644
  1629.9 322.0 %copy-start.24 = (f32[40,768]{1,0:T(8,128)S(1)}, f32[40,768]{1,0:T(8,128)}, u32[]{:S(2)}) copy-start(f32[40,768]{1,0:T(8,128)} %param.26) | copy-start | bytes 368644
  1630.3 320.8 %copy-start.48 = (f32[24,1280]{1,0:T(8,128)S(1)}, f32[24,1280]{1,0:T(8,128)}, u32[]{:S(2)}) copy-start(f32[24,1280]{1,0:T(8,128)} %param.33) | copy-start | bytes 368644
  1630.3 320.7 %copy-start.49 = (f32[24,1280]{1,0:T(8,128)S(1)}, f32[24,1280]{1,0:T(8,128)}, u32[]{:S(2)}) copy-start(f32[24,1280]{1,0:T(8,128)} %param.39) | copy-start | bytes 368644
  1630.3 321.5 %copy-start.50 = (f32[40,768]{1,0:T(8,128)S(1)}, f32[40,768]{1,0:T(8,128)}, u32[]{:S(2)}) copy-start(f32[40,768]{1,0:T(8,128)} %param.32) | copy-start | bytes 368644
  1630.3 321.5 %copy-start.51 = (f32[40,768]{1,0:T(8,128)S(1)}, f32[40,768]{1,0:T(8,128)}, u32[]{:S(2)}) copy-start(f32[40,768]{1,0:T(8,128)} %param.38) | copy-start | bytes 368644
  1630.4 323.2 %copy-start.14 = (f32[96,768]{1,0:T(8,128)S(1)}, f32[96,768]{1,0:T(8,128)}, u32[]{:S(2)}) copy-start(f32[96,768]{1,0:T(8,128)} %param.29) | copy-start | bytes 884740
  1630.4 323.2 %copy-start.28 = (f32[96,768]{1,0:T(8,128)S(1)}, f32[96,768]{1,0:T(8,128)}, u32[]{:S(2)}) copy-start(f32[96,768]{1,0:T(8,128)} %param.35) | copy-start | bytes 884740
  1630.4 323.2 %copy-start.29 = (f32[96,768]{1,0:T(8,128)S(1)}, f32[96,768]{1,0:T(8,128)}, u32[]{:S(2)}) copy-start(f32[96,768]{1,0:T(8,128)} %param.41) | copy-start | bytes 884740
  1630.4 325.2 %copy-start.16 = (f32[24,3072]{1,0:T(8,128)S(1)}, f32[24,3072]{1,0:T(8,128)}, u32[]{:S(2)}) copy-start(f32[24,3072]{1,0:T(8,128)} %param.28) | copy-start | bytes 884740
  1630.4 325.2 %copy-start.30 = (f32[24,3072]{1,0:T(8,128)S(1)}, f32[24,3072]{1,0:T(8,128)}, u32[]{:S(2)}) copy-start(f32[24,3072]{1,0:T(8,128)} %param.34) | copy-start | bytes 884740
  1630.4 325.2 %copy-start.31 = (f32[24,3072]{1,0:T(8,128)S(1)}, f32[24,3072]{1,0:T(8,128)}, u32[]{:S(2)}) copy-start(f32[24,3072]{1,0:T(8,128)} %param.40) | copy-start | bytes 884740
  (80 other events, 6505.8 us)
Sparse Core Ops, SparseCore 0:
  11.6 59.1 all-gather.5
  127.7 155.4 all-gather.7
  511.0 156.5 all-gather.9
  671.0 52.6 all-gather.11
  1038.6 158.2 reduce-scatter.7
  1293.2 159.4 all-reduce.4
  1458.6 193.5 reduce-scatter.11
  1658.2 135.1 reduce-scatter.9
  1798.8 103.4 reduce-scatter.5
where the time goes:
time: 1980 us; the launch traced here: 1970 us
  blocking collectives  540 us (27%)
  matrix products  519 us (26%)
  waiting for transfers between devices  475 us (24%)
  local copies, waits for them, and re-layouts  199 us (10%)
  other arithmetic  190 us (10%)
  between operations  23.3 us (1%)
  starting transfers between devices  20 us (1%)
    all_gather x1, blocking collectives, shards(): lax.all_gather(spectral_weight.astype(jnp.bfloat16), ('dp', 'wide'), axis...  215 us
    psum x1, blocking collectives, shards(): counts = lax.psum(local_counts, ('dp', 'wide'))  174 us
    reduce_scatter x1, waiting for transfers between devices, backward_layer(): lax.psum_scatter(grad_expand, ('dp', 'wide'), scatter_dimension=0, tiled=...  139 us
    all_to_all x1, waiting for transfers between devices, backward_layer(): lax.all_to_all(grad_cols, 'wide', split_axis=3, concat_axis=1, tiled=True)  139 us
    dot_general x1, matrix products, forward_layer(): jnp.dot(normed_two, expand_used, preferred_element_type=jnp.float32)  135 us
    all_to_all x1, waiting for transfers between devices, backward_layer(): lax.all_to_all(grad_rows, 'wide', split_axis=1, concat_axis=3, tiled=True)  115 us
    all_gather x1, blocking collectives, shards(): lax.all_gather(small_params.astype(jnp.bfloat16), ('dp', 'wide'), axis=1,...  70.5 us
    reduce_scatter x1, waiting for transfers between devices, backward_layer(): lax.psum_scatter(grad_embed, ('dp', 'wide'), scatter_dimension=0, tiled=T...  66.3 us
  transfers between devices with their start and end apart: 13, of which 5 were waited for; matrix products, arithmetic and copies ran while one was open for 36% of the time, Pallas kernels for 0%

commit v1 on v0

--- a/solution.py
+++ b/solution.py
@@ -9,6 +9,31 @@
 BETA_TWO = 0.95
 RATES = (0.08, 0.1, 0.1, 0.05, 0.3, 0.5)
 DECAYS = (0.1, 0.1, 0.1, 0.1, 0.1, 0.0)
+
+
+def raise_the_columns(patch, d0):
+    patch = jnp.moveaxis(patch, 0, d0)
+    passed = patch.shape
+    return patch.reshape(*passed[:d0], passed[d0] * passed[d0 + 1], *passed[d0 + 2 :])
+
+
+def stocks_arrange(local_array, dev_axis):
+    step_out = lax.axis_index(dev_axis)
+    g_now = lax.axis_size(dev_axis)
+    piece_out, side_arr = (g_now, step_out)
+    y1, z_new = (local_array[None], 1)
+    while z_new < piece_out:
+        pieces_in = []
+        pp = 0
+        while pp < piece_out:
+            pieces_in.append((pp, pp ^ z_new))
+            pp += 1
+        small = lax.ppermute(y1, dev_axis, pieces_in)
+        next_value = side_arr & z_new == 0
+        h_now = jnp.where(next_value, y1, small)
+        y1 = jnp.concatenate([h_now, jnp.where(next_value, small, y1)])
+        z_new *= 2
+    return y1
 
 
 def layer_norm(values, gain, shift):
@@ -283,12 +308,17 @@
         spectral_square,
         small_square,
     )
+
+    def serve_sources_all(row_data, vals, axis_no):
+        top = stocks_arrange(row_data, vals)
+        return raise_the_columns(top, axis_no)
+
     gathered = (
         lax.all_gather(embed_weight.astype(jnp.bfloat16), ("dp", "wide"), axis=0, tiled=True),
         lax.all_gather(head_weight.astype(jnp.bfloat16), ("dp", "wide"), axis=0, tiled=True),
         lax.all_gather(expand_weight.astype(jnp.bfloat16), ("dp", "wide"), axis=0, tiled=True),
         lax.all_gather(project_weight.astype(jnp.bfloat16), ("dp", "wide"), axis=0, tiled=True),
-        lax.all_gather(spectral_weight.astype(jnp.bfloat16), ("dp", "wide"), axis=2, tiled=True),
+        serve_sources_all(spectral_weight.astype(jnp.bfloat16), ("dp", "wide"), 2),
         lax.all_gather(small_params.astype(jnp.bfloat16), ("dp", "wide"), axis=1, tiled=True),
     )
     used = tuple(gathered[:5]) + (gathered[5].astype(jnp.float32),)

time: 1980 us -> 1910 us (0.965)
  blocking collectives: 540 us -> 329 us
  waiting for transfers between devices: 475 us -> 620 us
    all_gather x1 -> x0, blocking collectives: 215 us -> none  [shards(): lax.all_gather(spectral_weight.astype(jnp.bfloat16), ('dp', 'wide'), axis...]
    ppermute x0 -> x5, waiting for transfers between devices: none -> 147 us  [stocks_arrange(): small = lax.ppermute(y1, dev_axis, pieces_in)]
  transfers between devices with their start and end apart: 13 -> 18, of which waited for: 5 -> 10; matrix products, arithmetic and copies ran while one was open for 36% -> 37% of each run, Pallas kernels for 0% -> 0%
where the time goes in v1:
time: 1910 us; the launch traced here: 1900 us
  waiting for transfers between devices  620 us (32%)
  matrix products  502 us (26%)
  blocking collectives  329 us (17%)
  local copies, waits for them, and re-layouts  208 us (11%)
  other arithmetic  189 us (10%)
  starting transfers between devices  27.6 us (1%)
  between operations  23.3 us (1%)
    psum x1, blocking collectives, shards(): counts = lax.psum(local_counts, ('dp', 'wide'))  178 us
    ppermute x5, waiting for transfers between devices, stocks_arrange(): small = lax.ppermute(y1, dev_axis, pieces_in)  147 us
    reduce_scatter x1, waiting for transfers between devices, backward_layer(): lax.psum_scatter(grad_expand, ('dp', 'wide'), scatter_dimension=0, tiled=...  139 us
    all_to_all x1, waiting for transfers between devices, backward_layer(): lax.all_to_all(grad_cols, 'wide', split_axis=3, concat_axis=1, tiled=True)  139 us
    dot_general x1, matrix products, forward_layer(): jnp.dot(normed_two, expand_used, preferred_element_type=jnp.float32)  135 us
    all_to_all x1, waiting for transfers between devices, backward_layer(): lax.all_to_all(grad_rows, 'wide', split_axis=1, concat_axis=3, tiled=True)  115 us
    all_gather x1, blocking collectives, shards(): lax.all_gather(small_params.astype(jnp.bfloat16), ('dp', 'wide'), axis=1,...  70.5 us
    reduce_scatter x1, waiting for transfers between devices, backward_layer(): lax.psum_scatter(grad_embed, ('dp', 'wide'), scatter_dimension=0, tiled=T...  66.2 us
  transfers between devices with their start and end apart: 18, of which 10 were waited for; matrix products, arithmetic and copies ran while one was open for 37% of the time, Pallas kernels for 0%

profile of v1, /device:TPU:0, one launch (start us, length us, event | category | flops | bytes accessed | tf_op | source)
XLA Modules:
  0.0 1898.9 jit_solution(8991765838692902379)
XLA Ops:
  9.5 70.5 %all-gather = bf16[32,24,14]{1,2,0:T(8,128)(2,1)S(1)} all-gather(bf16[1,24,14]{1,2,0:T(8,128)(2,1)S(1)} %convert_bitcast_fusion.4), channel_id=1, replica_groups=mesh['dp'=4,'wide'=8] {'dp','wide'}, dimensions={0}, use_global_device_ids=true | all-gather | bytes 22176 | tf_op jit(solution)/shard_map/all_gather | solution.py:322
  125.6 46.6 %collective-permute-done = bf16[1,2,2,24,96]{4,3,0,2,1:T(8,128)(2,1)S(1)} collective-permute-done((bf16[1,2,2,24,96]{4,3,0,2,1:T(8,128)(2,1)S(1)}, bf16[1,2,2,24,96]{4,3,0,2,1:T(8,128)(2,1)S(1)}, u32[]{:S(2)}, u32[]{:S(2)}) %collective-permute-start) | collective-permute-done | bytes 18464 | tf_op jit(solution)/shard_map/ppermute | solution.py:31
  172.4 51.0 %collective-permute-done.1 = bf16[2,2,2,24,96]{4,3,0,2,1:T(8,128)(2,1)S(1)} collective-permute-done((bf16[2,2,2,24,96]{4,3,0,2,1:T(8,128)(2,1)S(1)}, bf16[2,2,2,24,96]{4,3,0,2,1:T(8,128)(2,1)S(1)}, u32[]{:S(2)}, u32[]{:S(2)}) %collective-permute-start.1) | collective-permute-done | bytes 36896 | tf_op jit(solution)/shard_map/ppermute | solution.py:31
  228.3 36.6 %collective-permute-done.2 = bf16[4,2,2,24,96]{4,3,0,2,1:T(8,128)(2,1)S(1)} collective-permute-done((bf16[4,2,2,24,96]{4,3,0,2,1:T(8,128)(2,1)S(1)}, bf16[4,2,2,24,96]{4,3,0,2,1:T(8,128)(2,1)S(1)}, u32[]{:S(2)}, u32[]{:S(2)}) %collective-permute-start.2) | collective-permute-done | bytes 73760 | tf_op jit(solution)/shard_map/ppermute | solution.py:31
  293.7 14.9 reshape.652
  320.5 12.9 convolution_bitcast_fusion.3
  358.8 14.9 slice_subtract_fusion.2
  424.6 15.6 copy.224
  446.7 178.4 %psum.22 = f32[20]{0:T(128)S(1)} all-reduce(f32[20]{0:T(128)S(1)} %broadcast_multiply_fusion.3), channel_id=1, replica_groups=mesh['dp'=4,'wide'=8] {'dp','wide'}, use_global_device_ids=true, to_apply=%region_9.10 | all-reduce | flops 20 | bytes 160 | tf_op jit(solution)/shard_map/psum | solution.py:335
  646.4 135.4 %multiply_convert_fusion = (bf16[4096,3072]{1,0:T(8,128)(2,1)}, f32[4096,3072]{1,0:T(8,128)}, f32[4096,3072]{1,0:T(8,128)}) fusion(f32[3072]{0:T(1024)S(1)} %add.414, bf16[768,3072]{1,0:T(8,128)(2,1)} %all-gather.8.cloned.1.call-done, f32[4096,768]{1,0:T(8,128)} %copy-done.1, f32[768]{0:T(1024)S(1)} %copy-done.85, f32[768]{0:T(1024)S(1)} %copy-done.67, ...), kind=kOutput, calls=%fused_computation.4 | convolution fusion | flops 20173553664 | bytes 143181824 | tf_op jit(solution)/shard_map/dot_general | solution.py:140
  781.9 27.6 %add_convert_fusion.2 = bf16[4096,768]{1,0:T(8,128)(2,1)} fusion(f32[4096,768]{1,0:T(8,128)} %copy-done.1, bf16[4096,3072]{1,0:T(8,128)(2,1)} %get-tuple-element.123, bf16[3072,768]{1,0:T(8,128)(2,1)} %all-gather.10.cloned.1.call-done, f32[768]{0:T(1024)S(1)} %copy-done.87), kind=kOutput, calls=%fused_computation.56 | convolution fusion | flops 19336790016 | bytes 48761856 | tf_op jit(solution)/shard_map/dot_general | solution.py:146
  809.6 16.8 fusion.10
  837.4 54.3 %convert_reduce_fusion = (f32[3072]{0:T(1024)}, bf16[4096,3072]{1,0:T(8,128)(2,1)}) fusion(f32[4096,3072]{1,0:T(8,128)} %get-tuple-element.124, bf16[3072,768]{1,0:T(8,128)(2,1)} %all-gather.10.cloned.1.call-done, f32[4096,768]{1,0:T(8,128)} %fusion.127, f32[4096,3072]{1,0:T(8,128)} %get-tuple-element.160, f32[3072]{0:T(1024)S(1)} %add.414), kind=kOutput, calls=%fused_computation.2 | convolution fusion | flops 19544403968 | bytes 143155200 | tf_op jit(solution)/shard_map/td,fd->tf/dot_general | solution.py:192
  891.7 27.8 %multiply_reduce_fusion = (f32[768]{0:T(1024)}, f32[4096]{0:T(1024)S(1)}, f32[768]{0:T(1024)}, f32[4096,768]{1,0:T(8,128)S(1)}) fusion(f32[4096,768]{1,0:T(8,128)} %copy-done.1, f32[4096]{0:T(1024)S(1)} %fusion.102, f32[4096]{0:T(1024)S(1)} %broadcast_multiply_fusion.1, f32[768]{0:T(1024)S(1)} %copy-done.67, bf16[4096,3072]{1,0:T(8,128)(2,1)} %get-tuple-element.163, ...), kind=kOutput, calls=%fused_computation.49 | convolution fusion | flops 19352514560 | bytes 55108608 | tf_op jit(solution)/shard_map/tf,df->td/dot_general | solution.py:199
  927.0 16.7 fusion.120
  945.6 15.6 copy.226
  966.6 13.9 fusion.129
  980.6 139.3 %all-to-all-done.2 = bf16[4,8,2,64,768]{4,2,1,0,3:T(2,128)(2,1)} async-done(((bf16[4,8,2,64,768]{4,2,1,0,3:T(2,128)(2,1)}), bf16[4,8,2,64,768]{4,2,1,0,3:T(2,128)(2,1)}, u32[]{:S(2)}, u32[]{:S(2)}) %all-to-all-start.2) | async-done | bytes 6291488 | tf_op jit(solution)/shard_map/all_to_all | solution.py:207
  1137.1 15.0 reshape.655
  1152.1 22.9 %fusion.68 = f32[2,2,8,96,96]{3,4,0,1,2:T(8,128)S(1)} fusion(bf16[256,2,8,8,96,1]{4,3,2,1,0,5:T(8,128)(2,1)} %bitcast.310, f32[256,1,8,8,96]{0,4,2,3,1:T(8,128)} %copy-done.2, f32[256,1,8,8,96]{0,4,2,3,1:T(8,128)} %copy-done.3, f32[2,8,96]{2,1,0:T(8,128)S(1)} %copy-done.36), kind=kOutput, calls=%fused_computation.120 | convolution fusion | flops 1220542464 | bytes 20060160 | tf_op jit(solution)/shard_map/xakbi,xokbj->aobij/dot_general | solution.py:99
  1175.9 23.1 %convolution_bitcast_fusion.1 = f32[256,2,2,8,8,96]{0,5,3,4,2,1:T(8,128)} fusion(bf16[2,8,96,96,1,1]{3,2,5,1,0,4:T(8,128)(2,1)S(1)} %bitcast.326, bf16[256,2,8,8,96,1]{4,3,2,1,0,5:T(8,128)(2,1)} %bitcast.311), kind=kOutput, calls=%fused_computation.66 | convolution fusion | flops 1207959552 | bytes 31752192 | tf_op jit(solution)/shard_map/xokbj,cbij->xockbi/dot_general | solution.py:93
  1226.6 28.8 %fusion.106 = f32[3072,768]{1,0:T(8,128)} fusion(bf16[4096,3072]{1,0:T(8,128)(2,1)} %get-tuple-element.123, f32[4096,768]{1,0:T(8,128)} %fusion.127), kind=kOutput, calls=%fused_computation.236 | convolution fusion | flops 19330498560 | bytes 47185920 | tf_op jit(solution)/shard_map/tf,td->fd/dot_general | solution.py:188
  1255.5 13.1 convolution_bitcast_fusion
  1311.1 15.7 copy.239
  1331.6 29.8 %fusion.111 = f32[768,3072]{1,0:T(8,128)} fusion(bf16[4096,3072]{1,0:T(8,128)(2,1)} %get-tuple-element.163, f32[4096,768]{1,0:T(8,128)} %copy-done.1, f32[768]{0:T(1024)S(1)} %copy-done.86, f32[768]{0:T(1024)S(1)} %copy-done.68, f32[4096]{0:T(1024)S(1)} %copy-done.59, f32[4096]{0:T(1024)S(1)} %copy-done.39), kind=kOutput, calls=%fused_computation.241 | convolution fusion | flops 19343081472 | bytes 47224832 | tf_op jit(solution)/shard_map/td,tf->df/dot_general | solution.py:197
  1361.5 114.6 %all-to-all-done.3 = bf16[4,64,2,8,768]{4,2,3,0,1:T(2,128)(2,1)} async-done(((bf16[4,64,2,8,768]{4,2,3,0,1:T(2,128)(2,1)}), bf16[4,64,2,8,768]{4,2,3,0,1:T(2,128)(2,1)}, u32[]{:S(2)}, u32[]{:S(2)}) %all-to-all-start.3) | async-done | bytes 6291488 | tf_op jit(solution)/shard_map/all_to_all | solution.py:221
  1486.1 20.9 %multiply_reduce_fusion.1 = (f32[768]{0:T(1024)S(1)}, f32[4096]{0:T(1024)S(1)}, f32[768]{0:T(1024)S(1)}, f32[4096,768]{1,0:T(8,128)}) fusion(f32[4096,768]{1,0:T(8,128)} %copy-done, f32[4096]{0:T(1024)S(1)} %copy-done.30, f32[4096]{0:T(1024)S(1)} %copy-done.22, f32[768]{0:T(1024)S(1)} %copy-done.45, f32[768]{0:T(1024)S(1)} %copy-done.57, ...), kind=kLoop, calls=%fused_computation.50 | loop fusion | flops 31451648 | bytes 50393088 | tf_op jit(solution)/shard_map/transpose(jvp())/reduce_sum | solution.py:42
  1571.1 13.6 reduce-scatter.12.cloned.1.call-done
  1586.4 139.4 %reduce-scatter.10.cloned.1.call-done = f32[24,3072]{1,0:T(8,128)} async-done(((f32[768,3072]{1,0:T(8,128)}), f32[24,3072]{1,0:T(8,128)}) %reduce-scatter.10.cloned.1.call-update) | async-done | bytes 294928 | tf_op jit(solution)/shard_map/reduce_scatter | solution.py:246
  1727.7 40.1 %all-reduce.1 = f32[14,768]{1,0:T(8,128)S(1)} all-reduce(f32[14,768]{1,0:T(8,128)S(1)} %concatenate.35), channel_id=7, replica_groups=mesh['dp'=4,'wide'=8] {'dp','wide'}, use_global_device_ids=true, to_apply=%region_34.35.clone | all-reduce | flops 10752 | bytes 86016
  1768.5 66.2 %reduce-scatter.6.cloned.1.call-done = f32[40,768]{1,0:T(8,128)} async-done(((f32[1280,768]{1,0:T(8,128)}), f32[40,768]{1,0:T(8,128)}) %reduce-scatter.6.cloned.1.call-update) | async-done | bytes 122896 | tf_op jit(solution)/shard_map/reduce_scatter | solution.py:244
  1840.1 39.8 %all-reduce.2 = (f32[20]{0:T(128)S(1)}, f32[]{:T(128)}) all-reduce(f32[20]{0:T(128)S(1)} %copy-done.90, f32[]{:T(128)S(6)} %add.440), channel_id=1, replica_groups=mesh['dp'=4,'wide'=8] {'dp','wide'}, use_global_device_ids=true, to_apply=%region_6.7 | all-reduce | flops 21 | bytes 168 | tf_op jit(solution)/shard_map/psum | solution.py:349
  (379 shorter events, 403.6 us)
Async XLA Ops:
  7.2 86.6 %all-gather.6.cloned.1.call-start = ((), (), s32[]{:S(2)}) async-start(), calls=%async_computation.8 | async-start | bytes 2027520 | tf_op jit(solution)/shard_map/all_gather | solution.py:317
  80.6 546.8 %copy-start.18 = (bf16[128,2,64]{0,2,1:T(8,128)(2,1)}, bf16[128,2,64]{0,2,1:T(8,128)(2,1)S(1)}, u32[]{:S(2)}) copy-start(bf16[128,2,64]{0,2,1:T(8,128)(2,1)S(1)} %fusion.80) | copy-start | bytes 98308
  81.3 550.9 %copy-start.44 = (f32[768]{0:T(1024)}, f32[768]{0:T(1024)S(1)}, u32[]{:S(2)}) copy-start(f32[768]{0:T(1024)S(1)} %get-tuple-element.91) | copy-start | bytes 9220
  81.3 550.9 %copy-start.56 = (f32[768]{0:T(1024)}, f32[768]{0:T(1024)S(1)}, u32[]{:S(2)}) copy-start(f32[768]{0:T(1024)S(1)} %get-tuple-element.90) | copy-start | bytes 9220
  105.6 526.6 %copy-start.21 = (f32[4096]{0:T(1024)}, f32[4096]{0:T(1024)S(1)}, u32[]{:S(2)}) copy-start(f32[4096]{0:T(1024)S(1)} %broadcast_multiply_fusion.2) | copy-start | bytes 49156
  107.5 524.7 %copy-start.29 = (f32[4096]{0:T(1024)}, f32[4096]{0:T(1024)S(1)}, u32[]{:S(2)}) copy-start(f32[4096]{0:T(1024)S(1)} %fusion.101) | copy-start | bytes 49156
  118.9 161.5 %all-to-all-start = ((bf16[4,8,2,64,768]{4,1,0,2,3:T(8,128)(2,1)}), bf16[4,8,2,64,768]{4,1,0,2,3:T(8,128)(2,1)}, u32[]{:S(2)}, u32[]{:S(2)}) async-start(bf16[4,8,2,64,768]{4,1,0,2,3:T(8,128)(2,1)} %copy.210), calls=%async_computation | async-start | bytes 12582912 | tf_op jit(solution)/shard_map/all_to_all | solution.py:123
  123.6 522.8 %all-gather.8.cloned.1.call-start = ((), (), s32[]{:S(2)}) async-start(), calls=%async_computation.9 | async-start | bytes 4866048 | tf_op jit(solution)/shard_map/all_gather | solution.py:319
  123.7 48.5 %collective-permute-start = (bf16[1,2,2,24,96]{4,3,0,2,1:T(8,128)(2,1)S(1)}, bf16[1,2,2,24,96]{4,3,0,2,1:T(8,128)(2,1)S(1)}, u32[]{:S(2)}, u32[]{:S(2)}) collective-permute-start(bf16[1,2,2,24,96]{4,3,0,2,1:T(8,128)(2,1)S(1)} %convert_bitcast_fusion.2), channel_id=1, source_target_pairs={{0,1},{1,0},{2,3},{3,2},{4,5},{5,4},{6,7},{7,6},{8,9},{9,8},{10,11... | collective-permute-start | bytes 55304 | tf_op jit(solution)/shard_map/ppermute | solution.py:31
  172.2 51.2 %collective-permute-start.1 = (bf16[2,2,2,24,96]{4,3,0,2,1:T(8,128)(2,1)S(1)}, bf16[2,2,2,24,96]{4,3,0,2,1:T(8,128)(2,1)S(1)}, u32[]{:S(2)}, u32[]{:S(2)}) collective-permute-start(bf16[2,2,2,24,96]{4,3,0,2,1:T(8,128)(2,1)S(1)} %pad_maximum_fusion.3), channel_id=1, source_target_pairs={{0,2},{1,3},{2,0},{3,1},{4,6},{5,7},{6,4},{7,5},{8,10},{9,11},{10,... | collective-permute-start | bytes 110600 | tf_op jit(solution)/shard_map/ppermute | solution.py:31
  223.5 41.4 %collective-permute-start.2 = (bf16[4,2,2,24,96]{4,3,0,2,1:T(8,128)(2,1)S(1)}, bf16[4,2,2,24,96]{4,3,0,2,1:T(8,128)(2,1)S(1)}, u32[]{:S(2)}, u32[]{:S(2)}) collective-permute-start(bf16[4,2,2,24,96]{4,3,0,2,1:T(8,128)(2,1)S(1)} %pad_maximum_fusion.2), channel_id=1, source_target_pairs={{0,4},{1,5},{2,6},{3,7},{4,0},{5,1},{6,2},{7,3},{8,12},{9,13},{10,... | collective-permute-start | bytes 221192 | tf_op jit(solution)/shard_map/ppermute | solution.py:31
  265.0 1.5 collective-permute-start.3
  266.6 13.3 collective-permute-start.4
  440.2 187.2 %all-to-all-start.1 = ((bf16[4,64,2,8,768]{4,2,3,0,1:T(2,128)(2,1)}), bf16[4,64,2,8,768]{4,2,3,0,1:T(2,128)(2,1)}, u32[]{:S(2)}, u32[]{:S(2)}) async-start(bf16[4,64,2,8,768]{4,2,3,0,1:T(2,128)(2,1)} %copy.224), calls=%async_computation.1 | async-start | bytes 12582912 | tf_op jit(solution)/shard_map/all_to_all | solution.py:134
  445.0 336.9 %all-gather.10.cloned.1.call-start = ((), (), s32[]{:S(2)}) async-start(), calls=%async_computation.10 | async-start | bytes 4866048 | tf_op jit(solution)/shard_map/all_gather | solution.py:320
  445.7 363.8 %all-gather.12.cloned.1.call-start = ((), (), s32[]{:S(2)}) async-start(), calls=%async_computation.11 | async-start | bytes 2027520 | tf_op jit(solution)/shard_map/all_gather | solution.py:318
  961.2 158.7 %all-to-all-start.2 = ((bf16[4,8,2,64,768]{4,2,1,0,3:T(2,128)(2,1)}), bf16[4,8,2,64,768]{4,2,1,0,3:T(2,128)(2,1)}, u32[]{:S(2)}, u32[]{:S(2)}) async-start(bf16[4,8,2,64,768]{4,2,1,0,3:T(2,128)(2,1)} %copy.226), calls=%async_computation.2 | async-start | bytes 12582912 | tf_op jit(solution)/shard_map/all_to_all | solution.py:207
  966.6 593.0 %reduce-scatter.8.cloned.1.call-start = ((), (), s32[]{:S(2)}) async-start(), calls=%async_computation.13 | async-start | bytes 4055040 | tf_op jit(solution)/shard_map/reduce_scatter | solution.py:245
  980.6 589.0 %all-reduce.5.cloned.1.call-start = ((), (), s32[]{:S(2)}) async-start(), calls=%async_computation.16 | async-start | bytes 3145728
  1226.6 358.2 %reduce-scatter.12.cloned.1.call-start = ((), (), s32[]{:S(2)}) async-start(), calls=%async_computation.15 | async-start | bytes 9732096 | tf_op jit(solution)/shard_map/reduce_scatter | solution.py:247
  1326.8 149.3 %all-to-all-start.3 = ((bf16[4,64,2,8,768]{4,2,3,0,1:T(2,128)(2,1)}), bf16[4,64,2,8,768]{4,2,3,0,1:T(2,128)(2,1)}, u32[]{:S(2)}, u32[]{:S(2)}) async-start(bf16[4,64,2,8,768]{4,2,3,0,1:T(2,128)(2,1)} %copy.239), calls=%async_computation.3 | async-start | bytes 12582912 | tf_op jit(solution)/shard_map/all_to_all | solution.py:221
  1331.5 394.3 %reduce-scatter.10.cloned.1.call-start = ((), (), s32[]{:S(2)}) async-start(), calls=%async_computation.14 | async-start | bytes 9732096 | tf_op jit(solution)/shard_map/reduce_scatter | solution.py:246
  1361.4 473.3 %reduce-scatter.6.cloned.1.call-start = ((), (), s32[]{:S(2)}) async-start(), calls=%async_computation.12 | async-start | bytes 4055040 | tf_op jit(solution)/shard_map/reduce_scatter | solution.py:244
  1563.7 320.5 %copy-start.25 = (f32[40,768]{1,0:T(8,128)S(1)}, f32[40,768]{1,0:T(8,128)}, u32[]{:S(2)}) copy-start(f32[40,768]{1,0:T(8,128)} %param.26) | copy-start | bytes 368644
  1564.1 320.0 %copy-start.54 = (f32[40,768]{1,0:T(8,128)S(1)}, f32[40,768]{1,0:T(8,128)}, u32[]{:S(2)}) copy-start(f32[40,768]{1,0:T(8,128)} %param.32) | copy-start | bytes 368644
  1564.1 320.0 %copy-start.55 = (f32[40,768]{1,0:T(8,128)S(1)}, f32[40,768]{1,0:T(8,128)}, u32[]{:S(2)}) copy-start(f32[40,768]{1,0:T(8,128)} %param.38) | copy-start | bytes 368644
  1564.2 321.7 %copy-start.15 = (f32[96,768]{1,0:T(8,128)S(1)}, f32[96,768]{1,0:T(8,128)}, u32[]{:S(2)}) copy-start(f32[96,768]{1,0:T(8,128)} %param.29) | copy-start | bytes 884740
  1564.2 321.7 %copy-start.31 = (f32[96,768]{1,0:T(8,128)S(1)}, f32[96,768]{1,0:T(8,128)}, u32[]{:S(2)}) copy-start(f32[96,768]{1,0:T(8,128)} %param.35) | copy-start | bytes 884740
  1564.2 321.7 %copy-start.32 = (f32[96,768]{1,0:T(8,128)S(1)}, f32[96,768]{1,0:T(8,128)}, u32[]{:S(2)}) copy-start(f32[96,768]{1,0:T(8,128)} %param.41) | copy-start | bytes 884740
  1564.2 323.7 %copy-start.17 = (f32[24,3072]{1,0:T(8,128)S(1)}, f32[24,3072]{1,0:T(8,128)}, u32[]{:S(2)}) copy-start(f32[24,3072]{1,0:T(8,128)} %param.28) | copy-start | bytes 884740
  1564.2 323.7 %copy-start.33 = (f32[24,3072]{1,0:T(8,128)S(1)}, f32[24,3072]{1,0:T(8,128)}, u32[]{:S(2)}) copy-start(f32[24,3072]{1,0:T(8,128)} %param.34) | copy-start | bytes 884740
  1564.2 323.7 %copy-start.34 = (f32[24,3072]{1,0:T(8,128)S(1)}, f32[24,3072]{1,0:T(8,128)}, u32[]{:S(2)}) copy-start(f32[24,3072]{1,0:T(8,128)} %param.40) | copy-start | bytes 884740
  (89 other events, 7872.6 us)
Sparse Core Ops, SparseCore 0:
  11.6 59.1 all-gather.5
  228.4 80.2 all-gather.7
  449.3 159.4 all-gather.9
  612.2 53.7 all-gather.11
  980.7 157.6 reduce-scatter.7
  1226.7 158.9 all-reduce.4
  1391.6 193.1 reduce-scatter.11
  1590.7 135.1 reduce-scatter.9
  1731.2 103.4 reduce-scatter.5
